TPU v7x, 32 devices: a whole 2x2x4 slice. The times are simulated.
32 devices in a mesh: dp: 8 (over z, y), tensor: 4 (over x, core).
Axes of the slice: x: 2, y: 2, z: 4, core: 2. Of those that a mesh axis runs over, the one named last changes fastest.
Arguments:
- attention: bfloat16 [4096, 4096], P('dp', 'tensor'), may hold values from -0.44921875 to 0.546875
- cotangent: bfloat16 [4096, 2048], P('dp', 'tensor'), may hold values from -0.5 to 1.5
- projection: bfloat16 [4096, 2048], P(None, 'tensor'), may hold values from -0.125 to 0.125
Outputs:
- input_grad: bfloat16 [4096, 4096], P('dp', 'tensor')
- combined: float32 [4096, 2048], P(None, 'tensor')
All inputs are finite; a program needn't handle non-finite values.
Results may differ from a plain program's by a relative error of at most 0.0004.
Values may be sent and summed in bfloat16 or wider, within the bound.
No kernel may reach another device: no remote copies, remote signals or barrier semaphores. Data moves between devices by JAX's collectives and lax.ppermute only.
A program may use at most 64 MiB of HBM per device.

v0:
```python
import jax
import jax.numpy as jnp
from jax import lax
from jax.sharding import PartitionSpec as P

epsilon = 1e-06


def swapped(value, axis, stride):
    mask = 2**stride
    pairs = [(source, source ^ mask) for source in range(lax.axis_size(axis))]
    return lax.ppermute(value, axis, pairs)


def level_totals(local_dots, depth):
    totals = lax.psum(local_dots, "tensor")
    for shift_bit in range(depth + 1):
        totals = totals + swapped(totals, "dp", shift_bit)
    return totals


def halving_merge(block):
    replica_count = lax.axis_size("dp")
    levels = replica_count.bit_length() - 1
    replica = lax.axis_index("dp")
    portion = block
    for depth in range(levels):
        halfway = portion.shape[0] // 2
        upper_bit = jnp.right_shift(replica, depth) & 1
        retained = lax.dynamic_slice_in_dim(portion, upper_bit * halfway, halfway, 0)
        outgoing = lax.dynamic_slice_in_dim(portion, (1 - upper_bit) * halfway, halfway, 0)
        incoming = swapped(outgoing, "dp", depth)
        is_lower = upper_bit == 0
        lower_vec = jnp.where(is_lower, retained, incoming)
        upper_vec = jnp.where(is_lower, incoming, retained)
        local_dots = jnp.stack(
            [
                jnp.sum(lower_vec * lower_vec),
                jnp.sum(upper_vec * upper_vec),
                jnp.sum(lower_vec * upper_vec),
            ]
        )
        totals = level_totals(local_dots, depth)
        lower_sq = totals[0] + epsilon
        upper_sq = totals[1] + epsilon
        cross = totals[2]
        portion = (1.0 - cross / (2.0 * lower_sq)) * lower_vec + (
            1.0 - cross / (2.0 * upper_sq)
        ) * upper_vec
    return (portion, levels)


def on_device(attention, cotangent, projection):
    own_rows = lax.all_to_all(projection, "tensor", split_axis=0, concat_axis=1, tiled=True)
    input_grad = lax.dot_general(
        lax.all_gather(cotangent, "tensor", axis=1, tiled=True),
        own_rows,
        (((1,), (1,)), ((), ())),
        preferred_element_type=jnp.float32,
    ).astype(jnp.bfloat16)
    grad_block = lax.dot_general(
        lax.all_gather(attention, "tensor", axis=1, tiled=True),
        cotangent,
        (((0,), (0,)), ((), ())),
        preferred_element_type=jnp.float32,
    )
    merged, levels = halving_merge(grad_block)
    gathered = lax.all_gather(merged, "dp", axis=0, tiled=True)
    col_width = merged.shape[1]
    shaped = gathered.reshape((2,) * levels + (merged.shape[0], col_width))
    order = tuple(range(levels - 1, -1, -1)) + (levels, levels + 1)
    combined = jnp.transpose(shaped, order).reshape(-1, col_width)
    return (input_grad, combined)


def solution(mesh):
    return jax.shard_map(
        on_device,
        mesh=mesh,
        in_specs=(P("dp", "tensor"), P("dp", "tensor"), P(None, "tensor")),
        out_specs=(P("dp", "tensor"), P(None, "tensor")),
        check_vma=False,
    )
```

profile of v0, /device:TPU:0, one launch (start us, length us, event | category | flops | bytes accessed | tf_op | source)
XLA Modules:
  0.0 463.0 jit_solution(12655495875147555903)
XLA Ops:
  7.2 0.0 all-gather.6.cloned.1.call-start
  7.2 0.7 all-gather.6.cloned.1.call-update
  7.9 0.0 all-gather.4.cloned.1.call-start
  8.0 38.8 %all-gather.6.cloned.1.call-done = bf16[512,4096]{1,0:T(8,128)(2,1)} async-done(((bf16[512,1024]{1,0:T(8,128)(2,1)}), bf16[512,4096]{1,0:T(8,128)(2,1)}) %all-gather.6.cloned.1.call-update) | async-done | bytes 4194320 | tf_op jit(solution)/shard_map/all_gather | solution.py:62
  46.7 4.7 %fusion.3 = f32[4096,512]{1,0:T(8,128)S(1)} fusion(bf16[512,4096]{1,0:T(8,128)(2,1)} %all-gather.6.cloned.1.call-done, bf16[512,512]{1,0:T(8,128)(2,1)} %param.4), kind=kOutput, calls=%fused_computation.28 | convolution fusion | flops 2147483648 | bytes 13107200 | tf_op jit(solution)/shard_map/dot_general | solution.py:61
  51.4 0.0 copy-start
  51.4 2.7 constant_dynamic-slice_fusion.2
  54.1 2.0 copy-done
  56.1 1.5 collective-permute-start
  57.6 91.6 %collective-permute-done = f32[2048,512]{1,0:T(8,128)} collective-permute-done((f32[2048,512]{1,0:T(8,128)}, f32[2048,512]{1,0:T(8,128)}, u32[]{:S(2)}, u32[]{:S(2)}) %collective-permute-start) | collective-permute-done | bytes 4194336 | tf_op jit(solution)/shard_map/ppermute | solution.py:12
  149.1 8.4 %multiply_reduce_fusion.2 = (f32[]{:T(128)}, f32[]{:T(128)}, f32[]{:T(128)}, f32[2048,512]{1,0:T(8,128)}, f32[2048,512]{1,0:T(8,128)}) fusion(f32[2048,512]{1,0:T(8,128)} %collective-permute-done, f32[4096,512]{1,0:T(8,128)} %copy-done, s32[]{:T(128)S(6)} %select_n.57, pred[]{:T(512)S(6)} %eq.11), kind=kLoop, calls=%fused_computation.3 | loop fusion | flops 8388605 | bytes 16777232 | tf_op jit(solution)/shard_map/reduce_sum | solution.py:38
  157.6 2.0 pad_maximum_fusion
  159.6 5.7 %psum.21 = f32[3]{0:T(128)S(1)} all-reduce(f32[3]{0:T(128)S(1)} %pad_maximum_fusion), channel_id=1, replica_groups=mesh['dp'=8,'tensor'=4] {'tensor'}, use_global_device_ids=true, to_apply=%region_3.4 | all-reduce | flops 3 | bytes 24 | tf_op jit(solution)/shard_map/psum | solution.py:16
  165.3 1.7 collective-permute-start.1
  167.0 1.9 collective-permute-done.1
  168.9 0.6 fusion.2
  171.9 4.5 multiply_add_fusion
  176.5 0.0 copy-start.1
  176.5 2.0 copy-done.1
  178.5 0.2 constant_dynamic-slice_fusion.1
  178.6 1.7 collective-permute-start.2
  180.4 0.0 all-gather.4.cloned.1.call-update
  180.4 0.0 all-gather.8.cloned.1.call-start
  180.5 44.5 %collective-permute-done.2 = f32[1024,512]{1,0:T(8,128)} collective-permute-done((f32[1024,512]{1,0:T(8,128)S(1)}, f32[1024,512]{1,0:T(8,128)}, u32[]{:S(2)}, u32[]{:S(2)}) %collective-permute-start.2) | collective-permute-done | bytes 2097184 | tf_op jit(solution)/shard_map/ppermute | solution.py:12
  225.0 4.8 %multiply_reduce_fusion.5 = (f32[]{:T(128)}, f32[]{:T(128)}, f32[]{:T(128)}, f32[1024,512]{1,0:T(8,128)S(1)}, f32[1024,512]{1,0:T(8,128)}) fusion(f32[1024,512]{1,0:T(8,128)} %collective-permute-done.2, f32[2048,512]{1,0:T(8,128)} %copy-done.1, s32[]{:T(128)S(6)} %select_n.61, pred[]{:T(512)S(6)} %eq.10), kind=kLoop, calls=%fused_computation.9 | loop fusion | flops 4194301 | bytes 8388625 | tf_op jit(solution)/shard_map/reduce_sum | solution.py:38
  229.7 1.9 pad_maximum_fusion.1
  231.7 5.7 %psum.22 = f32[3]{0:T(128)S(1)} all-reduce(f32[3]{0:T(128)S(1)} %pad_maximum_fusion.1), channel_id=1, replica_groups=mesh['dp'=8,'tensor'=4] {'tensor'}, use_global_device_ids=true, to_apply=%region_7.8 | all-reduce | flops 3 | bytes 24 | tf_op jit(solution)/shard_map/psum | solution.py:16
  237.4 1.7 collective-permute-start.3
  239.1 1.9 collective-permute-done.3
  241.0 1.7 collective-permute-start.4
  242.7 1.9 collective-permute-done.4
  244.6 0.6 fusion.1
  247.7 2.1 multiply_add_fusion.1
  249.8 0.0 copy-start.2
  249.8 1.3 copy-done.2
  251.2 0.1 constant_dynamic-slice_fusion
  251.2 2.7 collective-permute-start.5
  253.9 43.3 %collective-permute-done.5 = f32[512,512]{1,0:T(8,128)S(1)} collective-permute-done((f32[512,512]{1,0:T(8,128)S(1)}, f32[512,512]{1,0:T(8,128)S(1)}, u32[]{:S(2)}, u32[]{:S(2)}) %collective-permute-start.5) | collective-permute-done | bytes 1048608 | tf_op jit(solution)/shard_map/ppermute | solution.py:12
  297.2 2.2 multiply_reduce_fusion.8
  299.4 2.0 pad_maximum_fusion.2
  301.3 5.7 %psum.23 = f32[3]{0:T(128)S(1)} all-reduce(f32[3]{0:T(128)S(1)} %pad_maximum_fusion.2), channel_id=1, replica_groups=mesh['dp'=8,'tensor'=4] {'tensor'}, use_global_device_ids=true, to_apply=%region_11.12 | all-reduce | flops 3 | bytes 24 | tf_op jit(solution)/shard_map/psum | solution.py:16
  307.1 1.4 collective-permute-start.6
  308.5 2.2 collective-permute-done.6
  310.7 0.7 collective-permute-start.7
  311.4 2.8 collective-permute-done.7
  314.3 2.1 collective-permute-start.8
  316.4 2.4 collective-permute-done.8
  318.8 0.6 fusion
  321.8 1.2 multiply_add_fusion.2
  323.0 0.0 all-gather.8.cloned.1.call-update
  323.0 53.9 %all_to_all.19 = bf16[4,1024,512]{2,1,0:T(8,128)(2,1)} all-to-all(bf16[4,1024,512]{2,1,0:T(8,128)(2,1)} %bitcast.29), channel_id=1, replica_groups=mesh['dp'=8,'tensor'=4] {'tensor'}, dimensions={0} | all-to-all | bytes 8388608 | tf_op jit(solution)/shard_map/all_to_all | solution.py:54
  376.9 6.3 %copy.7 = bf16[1024,4,512]{0,2,1:T(8,128)(2,1)} copy(bf16[1024,4,512]{2,0,1:T(8,128)(2,1)} %bitcast.26) | data formatting | bytes 8388608 | tf_op jit(solution)/shard_map/all_to_all | solution.py:54
  383.2 0.0 all-gather.4.cloned.1.call-done
  383.2 6.1 %convolution_convert_fusion = bf16[512,1024]{1,0:T(8,128)(2,1)} fusion(bf16[512,2048]{1,0:T(8,128)(2,1)} %all-gather.4.cloned.1.call-done, bf16[1024,2048]{0,1:T(8,128)(2,1)} %bitcast.30), kind=kOutput, calls=%fused_computation.12 | convolution fusion | flops 2148007936 | bytes 7340032 | tf_op jit(solution)/shard_map/dot_general | solution.py:55
  389.3 59.4 %all-gather.8.cloned.1.call-done = f32[4096,512]{1,0:T(8,128)} async-done(((f32[512,512]{1,0:T(8,128)}), f32[4096,512]{1,0:T(8,128)}) %all-gather.8.cloned.1.call-update) | async-done | bytes 8388624 | tf_op jit(solution)/shard_map/all_gather | solution.py:68
  448.7 7.8 %copy.8 = f32[2,2,2,512,512]{4,3,2,1,0:T(8,128)} copy(f32[2,2,2,512,512]{4,3,0,1,2:T(8,128)} %bitcast.27) | data formatting | bytes 16777216 | tf_op jit(solution)/shard_map/transpose | solution.py:72
  (6 shorter events, 0.0 us)
Async XLA Ops:
  7.2 39.6 %all-gather.6.cloned.1.call-start = ((), (), s32[]{:S(2)}) async-start(), calls=%async_computation.2 | async-start | bytes 5242880 | tf_op jit(solution)/shard_map/all_gather | solution.py:62
  7.9 375.3 %all-gather.4.cloned.1.call-start = ((), (), s32[]{:S(2)}) async-start(), calls=%async_computation.1 | async-start | bytes 2621440 | tf_op jit(solution)/shard_map/all_gather | solution.py:56
  51.4 4.7 %copy-start = (f32[4096,512]{1,0:T(8,128)}, f32[4096,512]{1,0:T(8,128)S(1)}, u32[]{:S(2)}) copy-start(f32[4096,512]{1,0:T(8,128)S(1)} %fusion.3) | copy-start | bytes 25165828
  56.1 93.0 %collective-permute-start = (f32[2048,512]{1,0:T(8,128)}, f32[2048,512]{1,0:T(8,128)}, u32[]{:S(2)}, u32[]{:S(2)}) collective-permute-start(f32[2048,512]{1,0:T(8,128)} %constant_dynamic-slice_fusion.2), channel_id=1, source_target_pairs={{0,4},{4,0},{8,12},{12,8},{16,20},{20,16},{24,28},{28,24},{1,5},{5... | collective-permute-start | bytes 12582920 | tf_op jit(solution)/shard_map/ppermute | solution.py:12
  165.3 3.6 collective-permute-start.1
  176.5 2.0 copy-start.1
  178.6 46.3 %collective-permute-start.2 = (f32[1024,512]{1,0:T(8,128)S(1)}, f32[1024,512]{1,0:T(8,128)}, u32[]{:S(2)}, u32[]{:S(2)}) collective-permute-start(f32[1024,512]{1,0:T(8,128)S(1)} %constant_dynamic-slice_fusion.1), channel_id=1, source_target_pairs={{0,8},{4,12},{8,0},{12,4},{16,24},{20,28},{24,16},{28,20},{1,9},{5... | collective-permute-start | bytes 6291464 | tf_op jit(solution)/shard_map/ppermute | solution.py:12
  180.4 268.3 %all-gather.8.cloned.1.call-start = ((), (), s32[]{:S(2)}) async-start(), calls=%async_computation.3 | async-start | bytes 9437184 | tf_op jit(solution)/shard_map/all_gather | solution.py:68
  237.4 3.6 collective-permute-start.3
  241.0 3.6 collective-permute-start.4
  249.8 1.3 copy-start.2
  251.2 46.0 %collective-permute-start.5 = (f32[512,512]{1,0:T(8,128)S(1)}, f32[512,512]{1,0:T(8,128)S(1)}, u32[]{:S(2)}, u32[]{:S(2)}) collective-permute-start(f32[512,512]{1,0:T(8,128)S(1)} %constant_dynamic-slice_fusion), channel_id=1, source_target_pairs={{0,16},{4,20},{8,24},{12,28},{16,0},{20,4},{24,8},{28,12},{1,17},{... | collective-permute-start | bytes 3145736 | tf_op jit(solution)/shard_map/ppermute | solution.py:12
  307.1 3.6 collective-permute-start.6
  310.7 3.6 collective-permute-start.7
  314.3 4.5 collective-permute-start.8
Sparse Core Ops, SparseCore 0:
  9.5 37.1 all-gather.5
  180.5 21.7 all-gather.3
  323.1 125.5 all-gather.7
where the time goes:
time: 464 us; the launch traced here: 463 us
  waiting for transfers between devices  291 us (63%)
  blocking collectives  71.1 us (15%)
  other arithmetic  29.1 us (6%)
  local copies, waits for them, and re-layouts  24 us (5%)
  between operations  21.2 us (5%)
  starting transfers between devices  15.4 us (3%)
  matrix products  10.8 us (2%)
    ppermute x9, waiting for transfers between devices, swapped(): return lax.ppermute(value, axis, pairs)  192 us
    all_gather x1, waiting for transfers between devices, on_device(): gathered = lax.all_gather(merged, 'dp', axis=0, tiled=True)  59.4 us
    all_to_all x1, blocking collectives, on_device(): lax.all_to_all(projection, 'tensor', split_axis=0, concat_axis=1, tiled=T...  53.9 us
    all_gather x1, waiting for transfers between devices, on_device(): lax.all_gather(attention, 'tensor', axis=1, tiled=True)  38.8 us
    psum x3, blocking collectives, level_totals(): totals = lax.psum(local_dots, 'tensor')  17.2 us
    reduce_sum x3, other arithmetic, halving_merge(): jnp.sum(lower_vec * lower_vec)  15.4 us
    ppermute x9, starting transfers between devices, swapped(): return lax.ppermute(value, axis, pairs)  15.3 us
  transfers between devices with their start and end apart: 12, of which 11 were waited for; matrix products, arithmetic and copies ran while one was open for 6% of the time, Pallas kernels for 0%

commit v1 on v0

v1 whole, which is shorter than its diff:
```python
import jax
import jax.numpy as jnp
from jax import lax
from jax.sharding import PartitionSpec as P

epsilon = 1e-06


def merge_coefs(gram):
    n = gram.shape[0]
    coefs = [jnp.zeros((n,), jnp.float32).at[i].set(1.0) for i in range(n)]
    while len(coefs) > 1:
        merged = []
        for low, high in zip(coefs[0::2], coefs[1::2]):
            low_g = jnp.sum(gram * low[:, None], 0)
            high_g = jnp.sum(gram * high[:, None], 0)
            low_sq = jnp.maximum(jnp.sum(low_g * low), 0.0)
            high_sq = jnp.maximum(jnp.sum(high_g * high), 0.0)
            most = jnp.sqrt(low_sq) * jnp.sqrt(high_sq)
            cross = jnp.clip(jnp.sum(low_g * high), -most, most)
            merged.append(
                (1.0 - cross / (2.0 * (low_sq + epsilon))) * low
                + (1.0 - cross / (2.0 * (high_sq + epsilon))) * high
            )
        coefs = merged
    return coefs[0]


def on_device(attention, cotangent, projection):
    n, groups = lax.axis_size("dp"), lax.axis_size("tensor")
    rows = attention.shape[0]
    own_rows = lax.all_to_all(projection, "tensor", split_axis=0, concat_axis=1, tiled=True)
    input_grad = lax.dot_general(
        lax.all_gather(cotangent, "tensor", axis=1, tiled=True),
        own_rows,
        (((1,), (1,)), ((), ())),
        preferred_element_type=jnp.float32,
    ).astype(jnp.bfloat16)

    acts = lax.all_to_all(attention, "dp", split_axis=1, concat_axis=0, tiled=True)
    acts = lax.all_gather(acts, "tensor", axis=1, tiled=True)
    cots = lax.all_gather(cotangent, "dp", axis=0, tiled=True)
    features, columns = acts.shape[1], cots.shape[1]
    grads = [
        lax.dot_general(
            acts[s * rows : (s + 1) * rows],
            cots[s * rows : (s + 1) * rows],
            (((0,), (0,)), ((), ())),
            preferred_element_type=jnp.float32,
        )
        for s in range(n)
    ]
    gram = jnp.stack([jnp.stack([jnp.sum(grads[i] * grads[j]) for j in range(n)]) for i in range(n)])
    gram = lax.psum(gram, ("dp", "tensor"))
    coefs = merge_coefs(gram)
    bound = jnp.sum(jnp.abs(coefs) * jnp.sqrt(jnp.diagonal(gram)))
    scale = jnp.exp2(jnp.floor(jnp.log2(jnp.maximum(bound, 1e-30)))+1)
    piece = sum(coefs[s] * grads[s] for s in range(n))
    sent = (piece * (16384.0 / scale)).astype(jnp.float16)
    gathered = lax.all_gather(sent, "dp", axis=0)
    combined = gathered.astype(jnp.float32) * (scale / 16384.0)
    combined = combined.reshape(n, groups, features // groups, columns).transpose(1, 0, 2, 3).reshape(-1, columns)
    return (input_grad, combined)


def solution(mesh):
    return jax.shard_map(
        on_device,
        mesh=mesh,
        in_specs=(P("dp", "tensor"), P("dp", "tensor"), P(None, "tensor")),
        out_specs=(P("dp", "tensor"), P(None, "tensor")),
        check_vma=False,
    )
```

time: 464 us -> 368 us (0.79)
  waiting for transfers between devices: 291 us -> 84.6 us
  blocking collectives: 71.1 us -> 157 us
  local copies, waits for them, and re-layouts: 24 us -> 55.2 us
  other arithmetic: 29.1 us -> 16.3 us
  starting transfers between devices: 15.4 us -> 5.06 us
  matrix products: 10.8 us -> 19.8 us
  between operations: 21.2 us -> 29.1 us
    ppermute x9 -> x0, waiting for transfers between devices: 192 us -> none  [swapped(): return lax.ppermute(value, axis, pairs)]
    all_gather x0 -> x1, blocking collectives: none -> 84.7 us  [on_device(): gathered = lax.all_gather(sent, 'dp', axis=0)]
    all_gather x2, waiting for transfers between devices: 98.2 us -> 35 us  [the longest x1 35 us: on_device(): acts = lax.all_gather(acts, 'tensor', axis=1, tiled=True)]
    all_to_all x0 -> x1, waiting for transfers between devices: none -> 48.2 us  [on_device(): lax.all_to_all(projection, 'tensor', split_axis=0, concat_axis=1, tiled=T...]
    another operation x0 -> x9, local copies, waits for them, and re-layouts: none -> 40.4 us  [the longest x8 40.4 us: on_device(): jnp.stack([jnp.sum(grads[i] * grads[j]) for j in range(n)])]
    psum x3 -> x1, blocking collectives: 17.2 us -> 39.3 us  [on_device(): gram = lax.psum(gram, ('dp', 'tensor'))]
    all_to_all x1, blocking collectives: 53.9 us -> 32.9 us  [on_device(): lax.all_to_all(attention, 'dp', split_axis=1, concat_axis=0, tiled=True)]
    ppermute x9 -> x0, starting transfers between devices: 15.3 us -> none  [swapped(): return lax.ppermute(value, axis, pairs)]
  transfers between devices with their start and end apart: 12 -> 4, of which waited for: 11 -> 2; matrix products, arithmetic and copies ran while one was open for 6% -> 4% of each run, Pallas kernels for 0% -> 0%
where the time goes in v1:
time: 368 us; the launch traced here: 367 us
  blocking collectives  157 us (43%)
  waiting for transfers between devices  84.6 us (23%)
  local copies, waits for them, and re-layouts  55.2 us (15%)
  between operations  29.1 us (8%)
  matrix products  19.8 us (5%)
  other arithmetic  16.3 us (4%)
  starting transfers between devices  5.06 us (1%)
    all_gather x1, blocking collectives, on_device(): gathered = lax.all_gather(sent, 'dp', axis=0)  84.7 us
    all_to_all x1, waiting for transfers between devices, on_device(): lax.all_to_all(projection, 'tensor', split_axis=0, concat_axis=1, tiled=T...  48.2 us
    another operation x8, local copies, waits for them, and re-layouts, on_device(): jnp.stack([jnp.sum(grads[i] * grads[j]) for j in range(n)])  40.4 us
    psum x1, blocking collectives, on_device(): gram = lax.psum(gram, ('dp', 'tensor'))  39.3 us
    all_gather x1, waiting for transfers between devices, on_device(): acts = lax.all_gather(acts, 'tensor', axis=1, tiled=True)  35 us
    all_to_all x1, blocking collectives, on_device(): lax.all_to_all(attention, 'dp', split_axis=1, concat_axis=0, tiled=True)  32.9 us
    dot_general x8, matrix products, on_device(): lax.dot_general(acts[s * rows:(s + 1) * rows], cots[s * rows:(s + 1) * ro...  13.7 us
    convert_element_type x1, other arithmetic, on_device(): sent = (piece * (16384.0 / scale)).astype(jnp.float16)  8.49 us
  transfers between devices with their start and end apart: 4, of which 2 were waited for; matrix products, arithmetic and copies ran while one was open for 4% of the time, Pallas kernels for 0%

profile of v1, /device:TPU:0, one launch (start us, length us, event | category | flops | bytes accessed | tf_op | source)
XLA Modules:
  0.0 367.0 jit_solution(10417445836399652585)
XLA Ops:
  7.2 0.0 all-gather.6.cloned.1.call-start
  7.2 0.7 all-gather.6.cloned.1.call-update
  7.9 0.0 all-gather.10.cloned.1.call-start
  7.9 0.7 all-gather.10.cloned.1.call-update
  8.6 0.0 all-gather.8.cloned.1.call-start
  8.7 1.5 copy.8
  10.2 32.9 %all_to_all.38 = bf16[512,8,128]{0,2,1:T(8,128)(2,1)S(1)} all-to-all(bf16[512,8,128]{0,2,1:T(8,128)(2,1)S(1)} %bitcast.72), channel_id=1, replica_groups=mesh['dp'=8,'tensor'=4] {'dp'}, dimensions={1} | all-to-all | bytes 2097152 | tf_op jit(solution)/shard_map/all_to_all | solution.py:40
  43.1 1.3 copy.9
  44.4 0.0 all-gather.8.cloned.1.call-update
  44.4 5.0 %all-to-all-start = ((bf16[4,1024,512]{2,1,0:T(8,128)(2,1)}), bf16[4,1024,512]{2,1,0:T(8,128)(2,1)}, u32[]{:S(2)}, u32[]{:S(2)}) async-start(bf16[4,1024,512]{2,1,0:T(8,128)(2,1)} %bitcast.68), calls=%async_computation | async-start | bytes 8388608 | tf_op jit(solution)/shard_map/all_to_all | solution.py:32
  49.4 48.2 %all-to-all-done = bf16[4,1024,512]{2,1,0:T(8,128)(2,1)} async-done(((bf16[4,1024,512]{2,1,0:T(8,128)(2,1)}), bf16[4,1024,512]{2,1,0:T(8,128)(2,1)}, u32[]{:S(2)}, u32[]{:S(2)}) %all-to-all-start) | async-done | bytes 4194336 | tf_op jit(solution)/shard_map/all_to_all | solution.py:32
  97.6 6.2 %copy.7 = bf16[1024,4,512]{0,2,1:T(8,128)(2,1)} copy(bf16[1024,4,512]{2,0,1:T(8,128)(2,1)} %bitcast.1) | data formatting | bytes 8388608 | tf_op jit(solution)/shard_map/all_to_all | solution.py:32
  103.8 6.1 %convolution_convert_fusion = bf16[512,1024]{1,0:T(8,128)(2,1)} fusion(bf16[512,2048]{1,0:T(8,128)(2,1)} %all-gather.6.cloned.1.call-done, bf16[1024,2048]{0,1:T(8,128)(2,1)} %bitcast.69), kind=kOutput, calls=%fused_computation.2 | convolution fusion | flops 2148007936 | bytes 7340032 | tf_op jit(solution)/shard_map/dot_general | solution.py:33
  109.9 35.0 %all-gather.8.cloned.1.call-done = bf16[4096,512]{1,0:T(8,128)(2,1)} async-done(((bf16[4096,128]{1,0:T(8,128)(2,1)}), bf16[4096,512]{1,0:T(8,128)(2,1)}) %all-gather.8.cloned.1.call-update) | async-done | bytes 4194320 | tf_op jit(solution)/shard_map/all_gather | solution.py:41
  144.9 1.8 fusion.12
  146.7 2.4 fusion.15
  149.2 0.0 copy-done.12
  149.2 1.5 fusion.18
  150.7 1.5 fusion.21
  152.2 0.0 copy-done.13
  152.2 0.0 copy-start
  152.2 0.5 fusion.3
  152.7 0.0 copy-start.1
  152.7 0.5 fusion.6
  153.1 0.0 copy-start.2
  153.2 0.5 fusion.9
  153.6 0.0 copy-start.3
  153.6 0.0 copy-start.4
  153.6 0.0 copy-start.5
  153.7 0.0 copy-start.6
  153.7 0.0 copy-start.7
  153.7 0.0 copy-start.8
  153.7 0.0 copy-start.9
  153.7 0.0 copy-start.10
  153.7 0.0 copy-start.11
  153.7 5.1 %multiply_reduce_fusion = (f32[]{:T(128)}, f32[]{:T(128)}, f32[]{:T(128)}, f32[]{:T(128)}, f32[]{:T(128)}, /*index=5*/f32[]{:T(128)}, f32[]{:T(128)}, f32[]{:T(1...) fusion(f32[512,512]{1,0:T(8,128)S(1)} %fusion.3, ...), kind=kOutput, calls=%fused_computation.4 | convolution fusion | flops 287309824 | bytes 9437328 | tf_op jit(solution)/shard_map/dot_general | solution.py:45
  158.8 0.0 copy-done
  158.8 0.0 copy-done.1
  158.8 5.1 %stack.237 = f32[8]{0:T(128)S(1)} concatenate(f32[1]{0:T(128)} %bitcast.13, f32[1]{0:T(128)} %bitcast.21, f32[1]{0:T(128)} %bitcast.28, f32[1]{0:T(128)} %bitcast.34, f32[1]{0:T(128)} %bitcast.39, f32[1]{0:T(128)} %bitcast.43, f32[1]{0:T(128)} %bitcast.46, f32[1]{0:T(128)} %bitcast.48), dimensions={0} | concatenate | bytes 64 | tf_op jit(solution)/shard_map/stack | solution.py:53
  163.9 5.1 %stack.234 = f32[8]{0:T(128)S(1)} concatenate(f32[1]{0:T(128)} %bitcast.12, f32[1]{0:T(128)} %bitcast.20, f32[1]{0:T(128)} %bitcast.27, f32[1]{0:T(128)} %bitcast.33, f32[1]{0:T(128)} %bitcast.38, f32[1]{0:T(128)} %bitcast.42, f32[1]{0:T(128)} %bitcast.45, f32[1]{0:T(128)} %bitcast.46), dimensions={0} | concatenate | bytes 64 | tf_op jit(solution)/shard_map/stack | solution.py:53
  169.0 5.0 %stack.230 = f32[8]{0:T(128)S(1)} concatenate(f32[1]{0:T(128)} %bitcast.11, f32[1]{0:T(128)} %bitcast.19, f32[1]{0:T(128)} %bitcast.26, f32[1]{0:T(128)} %bitcast.32, f32[1]{0:T(128)} %bitcast.37, f32[1]{0:T(128)} %bitcast.41, f32[1]{0:T(128)} %bitcast.42, f32[1]{0:T(128)} %bitcast.43), dimensions={0} | concatenate | bytes 64 | tf_op jit(solution)/shard_map/stack | solution.py:53
  173.9 4.9 %stack.225 = f32[8]{0:T(128)S(1)} concatenate(f32[1]{0:T(128)} %bitcast.10, f32[1]{0:T(128)} %bitcast.18, f32[1]{0:T(128)} %bitcast.25, f32[1]{0:T(128)} %bitcast.31, f32[1]{0:T(128)} %bitcast.36, f32[1]{0:T(128)} %bitcast.37, f32[1]{0:T(128)} %bitcast.38, f32[1]{0:T(128)} %bitcast.39), dimensions={0} | concatenate | bytes 64 | tf_op jit(solution)/shard_map/stack | solution.py:53
  178.8 5.2 %stack.219 = f32[8]{0:T(128)S(1)} concatenate(f32[1]{0:T(128)} %bitcast.9, f32[1]{0:T(128)} %bitcast.17, f32[1]{0:T(128)} %bitcast.24, f32[1]{0:T(128)} %bitcast.30, f32[1]{0:T(128)} %bitcast.31, f32[1]{0:T(128)} %bitcast.32, f32[1]{0:T(128)} %bitcast.33, f32[1]{0:T(128)} %bitcast.34), dimensions={0} | concatenate | bytes 64 | tf_op jit(solution)/shard_map/stack | solution.py:53
  184.0 5.0 %stack.212 = f32[8]{0:T(128)S(1)} concatenate(f32[1]{0:T(128)} %bitcast.8, f32[1]{0:T(128)} %bitcast.16, f32[1]{0:T(128)} %bitcast.23, f32[1]{0:T(128)} %bitcast.24, f32[1]{0:T(128)} %bitcast.25, f32[1]{0:T(128)} %bitcast.26, f32[1]{0:T(128)} %bitcast.27, f32[1]{0:T(128)} %bitcast.28), dimensions={0} | concatenate | bytes 64 | tf_op jit(solution)/shard_map/stack | solution.py:53
  189.0 5.2 %stack.204 = f32[8]{0:T(128)S(1)} concatenate(f32[1]{0:T(128)} %bitcast.7, f32[1]{0:T(128)} %bitcast.15, f32[1]{0:T(128)} %bitcast.16, f32[1]{0:T(128)} %bitcast.17, f32[1]{0:T(128)} %bitcast.18, f32[1]{0:T(128)} %bitcast.19, f32[1]{0:T(128)} %bitcast.20, f32[1]{0:T(128)} %bitcast.21), dimensions={0} | concatenate | bytes 64 | tf_op jit(solution)/shard_map/stack | solution.py:53
  194.2 5.0 %stack.195 = f32[8]{0:T(128)S(1)} concatenate(f32[1]{0:T(128)} %bitcast.6, f32[1]{0:T(128)} %bitcast.7, f32[1]{0:T(128)} %bitcast.8, f32[1]{0:T(128)} %bitcast.9, f32[1]{0:T(128)} %bitcast.10, f32[1]{0:T(128)} %bitcast.11, f32[1]{0:T(128)} %bitcast.12, f32[1]{0:T(128)} %bitcast.13), dimensions={0} | concatenate | bytes 64 | tf_op jit(solution)/shard_map/stack | solution.py:53
  199.2 39.3 %psum.7 = f32[8,8]{1,0:T(8,128)S(1)} all-reduce(f32[8,8]{1,0:T(8,128)S(1)} %stack.239), channel_id=1, replica_groups=mesh['dp'=8,'tensor'=4] {'dp','tensor'}, use_global_device_ids=true, to_apply=%region_36.0 | all-reduce | flops 64 | bytes 512 | tf_op jit(solution)/shard_map/psum | solution.py:54
  238.6 0.0 copy-done.4
  238.6 0.0 copy-done.6
  238.6 0.1 multiply_reduce_fusion.48
  238.7 0.7 multiply_reduce_fusion.65
  242.1 0.7 multiply_reduce_fusion.55
  248.3 0.1 multiply_reduce_fusion.44
  248.4 0.7 multiply_reduce_fusion.63
  250.5 0.7 multiply_reduce_fusion.53
  253.9 0.1 multiply_reduce_fusion.36
  254.0 0.7 multiply_reduce_fusion.51
  256.8 0.6 gather_fusion
  257.4 0.6 multiply_reduce_fusion.50
  258.1 0.7 fusion.24
  259.5 8.5 %multiply_convert_fusion = f16[512,512]{1,0:T(8,128)(2,1)S(1)} fusion(f32[512,512]{1,0:T(8,128)} %get-tuple-element.179, f32[512,512]{1,0:T(8,128)} %copy-done.1, f32[512,512]{1,0:T(8,128)} %copy-done.2, f32[512,512]{1,0:T(8,128)} %copy-done.3, f32[512,512]{1,0:T(8,128)S(1)} %fusion.12, f32[512,512]{1,0:T(8,128)S(1)} %fusion.15, f32[512,512]{1,0:T(8,128)S(1)} %fusion.18, ...), kind=kLoop, calls=%fused_computation.3 | loop fusion | flops 4456448 | bytes 8912932 | tf_op jit(solution)/shard_map/convert_element_type | solution.py:59
  268.0 84.7 %all-gather.11 = f16[4096,512]{1,0:T(8,128)(2,1)} all-gather(f16[512,512]{1,0:T(8,128)(2,1)S(1)} %multiply_convert_fusion), channel_id=2, replica_groups=mesh['dp'=8,'tensor'=4] {'dp'}, dimensions={0}, use_global_device_ids=true | all-gather | bytes 4718592 | tf_op jit(solution)/shard_map/all_gather | solution.py:60
  352.7 3.4 convert_multiply_fusion
  356.1 4.4 %copy.10 = f32[4,8,128,512]{3,2,1,0:T(8,128)} copy(f32[4,8,128,512]{3,2,0,1:T(8,128)S(1)} %bitcast.66) | data formatting | bytes 16777216 | tf_op jit(solution)/shard_map/transpose | solution.py:62
  (20 shorter events, 0.1 us)
Async XLA Ops:
  7.2 96.6 %all-gather.6.cloned.1.call-start = ((), (), s32[]{:S(2)}) async-start(), calls=%async_computation.2 | async-start | bytes 2621440 | tf_op jit(solution)/shard_map/all_gather | solution.py:34
  7.9 102.0 %all-gather.10.cloned.1.call-start = ((), (), s32[]{:S(2)}) async-start(), calls=%async_computation.4 | async-start | bytes 4718592 | tf_op jit(solution)/shard_map/all_gather | solution.py:42
  8.6 136.3 %all-gather.8.cloned.1.call-start = ((), (), s32[]{:S(2)}) async-start(), calls=%async_computation.3 | async-start | bytes 5242880 | tf_op jit(solution)/shard_map/all_gather | solution.py:41
  44.4 53.2 %all-to-all-start = ((bf16[4,1024,512]{2,1,0:T(8,128)(2,1)}), bf16[4,1024,512]{2,1,0:T(8,128)(2,1)}, u32[]{:S(2)}, u32[]{:S(2)}) async-start(bf16[4,1024,512]{2,1,0:T(8,128)(2,1)} %bitcast.68), calls=%async_computation | async-start | bytes 8388608 | tf_op jit(solution)/shard_map/all_to_all | solution.py:32
  144.9 4.2 %copy-start.12 = (bf16[4096,512]{1,0:T(8,128)(2,1)S(1)}, bf16[4096,512]{1,0:T(8,128)(2,1)}, u32[]{:S(2)}) copy-start(bf16[4096,512]{1,0:T(8,128)(2,1)} %all-gather.10.cloned.1.call-done) | copy-start | bytes 12582916
  144.9 7.3 %copy-start.13 = (bf16[4096,512]{1,0:T(8,128)(2,1)S(1)}, bf16[4096,512]{1,0:T(8,128)(2,1)}, u32[]{:S(2)}) copy-start(bf16[4096,512]{1,0:T(8,128)(2,1)} %all-gather.8.cloned.1.call-done) | copy-start | bytes 12582916
  152.2 6.6 %copy-start = (f32[512,512]{1,0:T(8,128)}, f32[512,512]{1,0:T(8,128)S(1)}, u32[]{:S(2)}) copy-start(f32[512,512]{1,0:T(8,128)S(1)} %fusion.21) | copy-start | bytes 3145732
  152.7 6.1 %copy-start.1 = (f32[512,512]{1,0:T(8,128)}, f32[512,512]{1,0:T(8,128)S(1)}, u32[]{:S(2)}) copy-start(f32[512,512]{1,0:T(8,128)S(1)} %fusion.3) | copy-start | bytes 3145732
  153.1 5.7 %copy-start.2 = (f32[512,512]{1,0:T(8,128)}, f32[512,512]{1,0:T(8,128)S(1)}, u32[]{:S(2)}) copy-start(f32[512,512]{1,0:T(8,128)S(1)} %fusion.6) | copy-start | bytes 3145732
  153.6 5.2 %copy-start.3 = (f32[512,512]{1,0:T(8,128)}, f32[512,512]{1,0:T(8,128)S(1)}, u32[]{:S(2)}) copy-start(f32[512,512]{1,0:T(8,128)S(1)} %fusion.9) | copy-start | bytes 3145732
  153.6 84.9 %copy-start.4 = (f32[8]{0:T(128)S(1)}, f32[8]{0:T(128)}, u32[]{:S(2)}) copy-start(f32[8]{0:T(128)} %constant.225.clone.1) | copy-start | bytes 100
  153.6 84.9 %copy-start.5 = (f32[8]{0:T(128)S(1)}, f32[8]{0:T(128)}, u32[]{:S(2)}) copy-start(f32[8]{0:T(128)} %constant.226.clone.1) | copy-start | bytes 100
  153.7 84.9 %copy-start.6 = (f32[8]{0:T(128)S(1)}, f32[8]{0:T(128)}, u32[]{:S(2)}) copy-start(f32[8]{0:T(128)} %constant.223.clone.1) | copy-start | bytes 100
  153.7 84.9 %copy-start.7 = (f32[8]{0:T(128)S(1)}, f32[8]{0:T(128)}, u32[]{:S(2)}) copy-start(f32[8]{0:T(128)} %constant.224.clone.1) | copy-start | bytes 100
  153.7 84.9 %copy-start.8 = (f32[8]{0:T(128)S(1)}, f32[8]{0:T(128)}, u32[]{:S(2)}) copy-start(f32[8]{0:T(128)} %constant.217.clone.1) | copy-start | bytes 100
  153.7 84.9 %copy-start.9 = (f32[8]{0:T(128)S(1)}, f32[8]{0:T(128)}, u32[]{:S(2)}) copy-start(f32[8]{0:T(128)} %constant.221.clone.1) | copy-start | bytes 100
  153.7 84.9 %copy-start.10 = (f32[8]{0:T(128)S(1)}, f32[8]{0:T(128)}, u32[]{:S(2)}) copy-start(f32[8]{0:T(128)} %constant.222.clone.1) | copy-start | bytes 100
  153.7 84.9 %copy-start.11 = (f32[8]{0:T(128)S(1)}, f32[8]{0:T(128)}, u32[]{:S(2)}) copy-start(f32[8]{0:T(128)} %constant.218.clone.1) | copy-start | bytes 100
Sparse Core Ops, SparseCore 0:
  9.5 25.2 all-gather.5
  37.0 72.7 all-gather.9
  111.4 33.5 all-gather.7
